TPU v7x, 256 devices: a whole 4x4x8 slice. The times are simulated.
256 devices in a mesh: rep: 4 (over x), ep: 64 (over z, y, core).
Axes of the slice: x: 4, y: 4, z: 8, core: 2. Of those that a mesh axis runs over, the one named last changes fastest.
Arguments:
- out_grad: bfloat16 [16384, 2048], P(('rep', 'ep')), may hold values from -3 to 3
- saved_hidden: bfloat16 [16384, 2, 7168], P(('rep', 'ep')), may hold values from -0.59765625 to 0.59765625
- combine: bfloat16 [16384, 2], P(('rep', 'ep')), may hold values from 0.049804688 to 1
- expert_ids: int32 [16384, 2], P(('rep', 'ep')), may hold values from 0 to 7, all different within a row; in each aligned block of 64 rows (0 to 63, 64 to 127, ...) at most 24 rows name the same one
Outputs:
- down_grad: float32 [57344, 2048], P('ep', 'rep')
Inputs may be any that keep to these rules, and one draw needn't show every extreme that they name: `expert_ids`: in each aligned block of 64 rows (the rows of one device), no expert is named by more than 24 slots, a bound that some block reaches; the 2 ids of a row differ; every expert is named somewhere.
All inputs are finite; a program needn't handle non-finite values.
Results may differ from a plain program's by a relative error of at most 0.0042.
Values may be sent and summed in bfloat16 or wider, within the bound.
No kernel may reach another device: no remote copies, remote signals or barrier semaphores. Data moves between devices by JAX's collectives and lax.ppermute only.
A program may use at most 64 MiB of HBM per device.

v0:
```python
import jax
import jax.numpy as jnp
from jax import lax
from jax.sharding import PartitionSpec as P

EXPERTS = 8
TOP = 2
CAP = 24


def cut_along(array, dim, count):
    lengths = array.shape
    pieces = array.reshape(*lengths[:dim], count, lengths[dim] // count, *lengths[dim + 1 :])
    return jnp.moveaxis(pieces, dim, 0)


def summed_on_arrival(array, axis, dim):
    pieces = cut_along(array, dim, lax.axis_size(axis))
    arrived = lax.all_to_all(pieces, axis, split_axis=0, concat_axis=0, tiled=True)
    return arrived.astype(jnp.float32).sum(axis=0)


def per_device(out_grad, saved_hidden, combine, expert_ids):
    ep_count = lax.axis_size("ep")
    group_size = ep_count // EXPERTS
    tok_count = out_grad.shape[0]
    slot_count = tok_count * TOP
    unit_cols = saved_hidden.shape[2] // group_size
    model_width = out_grad.shape[1]
    flat_ids = expert_ids.reshape(slot_count)
    onehot = (flat_ids[:, None] == jnp.arange(EXPERTS, dtype=jnp.int32)[None, :]).astype(jnp.int32)
    slot_place = jnp.sum((jnp.cumsum(onehot, axis=0) - 1) * onehot, axis=1)
    slot_grad = jnp.broadcast_to(out_grad[:, None, :], (tok_count, TOP, model_width)).reshape(
        slot_count, model_width
    )
    send_grad = (
        jnp.zeros((EXPERTS, CAP, model_width), jnp.bfloat16).at[flat_ids, slot_place].set(slot_grad)
    )
    send_grad = jnp.broadcast_to(
        send_grad[:, None], (EXPERTS, group_size, CAP, model_width)
    ).reshape(ep_count, CAP, model_width)
    hidden_pieces = saved_hidden.reshape(slot_count, group_size, unit_cols)
    send_hidden = (
        jnp.zeros((EXPERTS, group_size, CAP, unit_cols), jnp.bfloat16)
        .at[flat_ids, :, slot_place, :]
        .set(hidden_pieces)
    )
    slot_prob = jnp.broadcast_to(combine.reshape(slot_count)[:, None], (slot_count, group_size))
    send_prob = (
        jnp.zeros((EXPERTS, group_size, CAP), jnp.bfloat16)
        .at[flat_ids, :, slot_place]
        .set(slot_prob)
    )
    recv_grad, recv_hidden, recv_prob = (
        lax.all_to_all(send_grad, "ep", split_axis=0, concat_axis=0, tiled=True),
        lax.all_to_all(
            send_hidden.reshape(ep_count, CAP, unit_cols),
            "ep",
            split_axis=0,
            concat_axis=0,
            tiled=True,
        ),
        lax.all_to_all(
            send_prob.reshape(ep_count, CAP), "ep", split_axis=0, concat_axis=0, tiled=True
        ),
    )
    row_total = ep_count * CAP
    grad_rows = recv_grad.reshape(row_total, model_width)
    hidden_rows = recv_hidden.reshape(row_total, unit_cols)
    prob_rows = recv_prob.reshape(row_total)
    scaled_all = (prob_rows[:, None].astype(jnp.float32) * grad_rows.astype(jnp.float32)).astype(
        jnp.bfloat16
    )
    contract_rows = (((0,), (0,)), ((), ()))
    weight_part = lax.dot_general(
        hidden_rows, scaled_all, contract_rows, preferred_element_type=jnp.float32
    )
    down_grad = summed_on_arrival(weight_part.astype(jnp.bfloat16), "rep", 1)
    return down_grad


def solution(mesh):
    in_specs = (
        P(("rep", "ep"), None),
        P(("rep", "ep"), None, None),
        P(("rep", "ep"), None),
        P(("rep", "ep"), None),
    )
    out_specs = P("ep", "rep")
    return jax.shard_map(
        per_device, mesh=mesh, in_specs=in_specs, out_specs=out_specs, check_vma=False
    )
```

profile of v0, /device:TPU:40, one launch (start us, length us, event | category | flops | bytes accessed | tf_op | source)
XLA Modules:
  0.0 326.8 jit_solution(11627005940811721644)
XLA Ops:
  0.0 0.8 copy.24
  0.8 0.1 eq.15
  0.9 0.1 reshape.85
  1.0 0.1 fusion.2
  1.1 0.2 reduce_window_sum.11
  1.3 0.2 select_reduce_fusion
  1.5 0.8 copy.27
  2.3 0.1 broadcast_in_dim.16
  2.4 0.1 broadcast_in_dim.17
  2.5 7.1 %scatter_fusion.1 = bf16[8,8,24]{1,2,0:T(8,128)(2,1)S(1)} fusion(bf16[8,8,24]{1,2,0:T(8,128)(2,1)S(1)} %broadcast_in_dim.15, s32[128]{0:T(128)S(1)} %fusion.4, bf16[128,8]{1,0:T(8,128)(2,1)S(1)} %broadcast_in_dim.17), kind=kCustom, calls=%fused_computation.1 | custom fusion | bytes 7168 | tf_op jit(solution)/shard_map/scatter | solution.py:52
  9.6 0.1 copy.28
  9.7 0.6 copy.29
  10.4 11.7 %all-to-all-start.1 = ((bf16[64,1,24]{2,1,0:T(2,128)(2,1)}), bf16[64,1,24]{2,1,0:T(2,128)(2,1)S(1)}, u32[]{:S(2)}, u32[]{:S(2)}) async-start(bf16[64,1,24]{2,1,0:T(2,128)(2,1)} %copy.29), calls=%async_computation.1 | async-start | bytes 65536 | tf_op jit(solution)/shard_map/all_to_all | solution.py:63
  22.0 5.4 %reshape.94 = bf16[128,8,896]{2,1,0:T(8,128)(2,1)} reshape(bf16[64,2,7168]{2,1,0:T(2,128)(2,1)} %param.5) | data formatting | bytes 3670016 | tf_op jit(solution)/shard_map/reshape | solution.py:42
  27.4 0.3 broadcast_in_dim.14
  27.7 13.2 %scatter_fusion = bf16[8,8,24,896]{3,1,2,0:T(8,128)(2,1)S(1)} fusion(bf16[8,8,24,896]{3,1,2,0:T(8,128)(2,1)S(1)} %broadcast_in_dim.14, s32[128]{0:T(128)S(1)} %fusion.4, bf16[128,8,896]{2,1,0:T(8,128)(2,1)} %reshape.94), kind=kCustom, calls=%fused_computation | custom fusion | bytes 5506048 | tf_op jit(solution)/shard_map/scatter | solution.py:46
  40.9 1.9 copy.26
  42.9 0.0 copy-start
  42.9 0.0 all-to-all-done.1
  42.9 0.0 copy-start.1
  42.9 0.6 copy-done.1
  43.5 10.3 %all-to-all-start = ((bf16[64,24,896]{2,1,0:T(8,128)(2,1)}), bf16[64,24,896]{2,1,0:T(8,128)(2,1)S(1)}, u32[]{:S(2)}, u32[]{:S(2)}) async-start(bf16[64,24,896]{2,1,0:T(8,128)(2,1)} %bitcast.22), calls=%async_computation | async-start | bytes 5505024 | tf_op jit(solution)/shard_map/all_to_all | solution.py:56
  53.8 0.0 copy-done
  53.8 0.3 broadcast_in_dim.19
  54.1 1.0 reshape.106
  55.1 0.1 broadcast_in_dim.18
  55.2 17.0 %scatter_fusion.2 = bf16[8,24,2048]{2,1,0:T(8,128)(2,1)S(1)} fusion(bf16[8,24,2048]{2,1,0:T(8,128)(2,1)S(1)} %broadcast_in_dim.18, s32[128]{0:T(128)S(1)} %fusion.4, bf16[128,2048]{1,0:T(8,128)(2,1)} %reshape.106), kind=kCustom, calls=%fused_computation.2 | custom fusion | bytes 1573888 | tf_op jit(solution)/shard_map/scatter | solution.py:37
  72.2 46.0 %all-to-all-done = bf16[64,24,896]{2,1,0:T(8,128)(2,1)S(1)} async-done(((bf16[64,24,896]{2,1,0:T(8,128)(2,1)}), bf16[64,24,896]{2,1,0:T(8,128)(2,1)S(1)}, u32[]{:S(2)}, u32[]{:S(2)}) %all-to-all-start) | async-done | bytes 2752544 | tf_op jit(solution)/shard_map/all_to_all | solution.py:56
  118.2 3.5 %broadcast_in_dim.20 = bf16[8,8,24,2048]{3,2,1,0:T(8,128)(2,1)} broadcast(bf16[8,24,2048]{2,1,0:T(8,128)(2,1)S(1)} %scatter_fusion.2), dimensions={0,2,3} | broadcast | bytes 7077888 | tf_op jit(solution)/shard_map/broadcast_in_dim | solution.py:39
  121.7 0.0 copy-start.2
  121.7 6.7 %all-to-all-start.2 = ((bf16[64,24,2048]{2,1,0:T(8,128)(2,1)}), bf16[64,24,2048]{2,1,0:T(8,128)(2,1)}, u32[]{:S(2)}, u32[]{:S(2)}) async-start(bf16[64,24,2048]{2,1,0:T(8,128)(2,1)} %bitcast.20), calls=%async_computation.2 | async-start | bytes 12582912 | tf_op jit(solution)/shard_map/all_to_all | solution.py:55
  128.4 0.0 copy-done.2
  128.4 140.5 %all-to-all-done.2 = bf16[64,24,2048]{2,1,0:T(8,128)(2,1)} async-done(((bf16[64,24,2048]{2,1,0:T(8,128)(2,1)}), bf16[64,24,2048]{2,1,0:T(8,128)(2,1)}, u32[]{:S(2)}, u32[]{:S(2)}) %all-to-all-start.2) | async-done | bytes 6291488 | tf_op jit(solution)/shard_map/all_to_all | solution.py:55
  268.9 8.4 %bitcast_convert_fusion = bf16[896,2048]{1,0:T(8,128)(2,1)S(1)} fusion(bf16[64,24,896]{2,1,0:T(8,128)(2,1)S(1)} %all-to-all-done, bf16[64,24,2048]{2,1,0:T(8,128)(2,1)} %all-to-all-done.2, f32[64,24]{1,0:T(8,128)S(1)} %bitcast.25), kind=kOutput, calls=%fused_computation.4 | convolution fusion | flops 5648416768 | bytes 12720128 | tf_op jit(solution)/shard_map/dot_general | solution.py:75
  277.3 0.3 copy.33
  277.7 47.3 %all_to_all.24 = bf16[4,896,512]{2,1,0:T(8,128)(2,1)S(1)} all-to-all(bf16[4,896,512]{2,1,0:T(8,128)(2,1)S(1)} %bitcast.21), channel_id=1, replica_groups=mesh['rep'=4,'ep'=64] {'rep'}, dimensions={0} | all-to-all | bytes 7340032 | tf_op jit(solution)/shard_map/all_to_all | solution.py:19
  325.0 1.8 convert_reduce_fusion
  (3 shorter events, 0.1 us)
Async XLA Ops:
  10.4 32.5 %all-to-all-start.1 = ((bf16[64,1,24]{2,1,0:T(2,128)(2,1)}), bf16[64,1,24]{2,1,0:T(2,128)(2,1)S(1)}, u32[]{:S(2)}, u32[]{:S(2)}) async-start(bf16[64,1,24]{2,1,0:T(2,128)(2,1)} %copy.29), calls=%async_computation.1 | async-start | bytes 65536 | tf_op jit(solution)/shard_map/all_to_all | solution.py:63
  42.9 10.9 %copy-start = (bf16[64,2048]{1,0:T(8,128)(2,1)S(1)}, bf16[64,2048]{1,0:T(8,128)(2,1)}, u32[]{:S(2)}) copy-start(bf16[64,2048]{1,0:T(8,128)(2,1)} %param.4) | copy-start | bytes 786436
  42.9 0.6 copy-start.1
  43.5 74.7 %all-to-all-start = ((bf16[64,24,896]{2,1,0:T(8,128)(2,1)}), bf16[64,24,896]{2,1,0:T(8,128)(2,1)S(1)}, u32[]{:S(2)}, u32[]{:S(2)}) async-start(bf16[64,24,896]{2,1,0:T(8,128)(2,1)} %bitcast.22), calls=%async_computation | async-start | bytes 5505024 | tf_op jit(solution)/shard_map/all_to_all | solution.py:56
  121.7 6.7 %copy-start.2 = (bf16[64,1,24]{2,1,0:T(2,128)(2,1)S(1)}, bf16[64,1,24]{2,1,0:T(2,128)(2,1)}, u32[]{:S(2)}) copy-start(bf16[64,1,24]{2,1,0:T(2,128)(2,1)} %copy-done.1) | copy-start | bytes 9220
  121.7 147.2 %all-to-all-start.2 = ((bf16[64,24,2048]{2,1,0:T(8,128)(2,1)}), bf16[64,24,2048]{2,1,0:T(8,128)(2,1)}, u32[]{:S(2)}, u32[]{:S(2)}) async-start(bf16[64,24,2048]{2,1,0:T(8,128)(2,1)} %bitcast.20), calls=%async_computation.2 | async-start | bytes 12582912 | tf_op jit(solution)/shard_map/all_to_all | solution.py:55
where the time goes:
time: 328 us; the launch traced here: 327 us
  waiting for transfers between devices  186 us (57%)
  local copies, waits for them, and re-layouts  53.5 us (16%)
  blocking collectives  47.3 us (14%)
  starting transfers between devices  28.7 us (9%)
  matrix products  8.38 us (3%)
    all_to_all x1, waiting for transfers between devices, per_device(): lax.all_to_all(send_grad, 'ep', split_axis=0, concat_axis=0, tiled=True)  140 us
    all_to_all x1, blocking collectives, summed_on_arrival(): lax.all_to_all(pieces, axis, split_axis=0, concat_axis=0, tiled=True)  47.3 us
    all_to_all x1, waiting for transfers between devices, per_device(): lax.all_to_all(send_hidden.reshape(ep_count, CAP, unit_cols), 'ep', split...  46 us
    scatter x1, local copies, waits for them, and re-layouts, per_device(): jnp.zeros((EXPERTS, CAP, model_width), jnp.bfloat16)  17 us
    scatter x2, local copies, waits for them, and re-layouts, per_device(): send_hidden = jnp.zeros((EXPERTS, group_size, CAP, unit_cols), jnp.bfloat...  15.1 us
    all_to_all x1, starting transfers between devices, per_device(): lax.all_to_all(send_prob.reshape(ep_count, CAP), 'ep', split_axis=0, conc...  11.7 us
    all_to_all x1, starting transfers between devices, per_device(): lax.all_to_all(send_hidden.reshape(ep_count, CAP, unit_cols), 'ep', split...  10.3 us
    dot_general x1, matrix products, per_device(): lax.dot_general(hidden_rows, scaled_all, contract_rows, preferred_element...  8.38 us
  transfers between devices with their start and end apart: 3, of which 2 were waited for; matrix products, arithmetic and copies ran while one was open for 12% of the time, Pallas kernels for 0%

commit v1 on v0

v1 whole, which is shorter than its diff:
```python
import functools

import jax
import jax.numpy as jnp
from jax import lax
from jax.experimental import pallas as pl
from jax.experimental.pallas import tpu as pltpu
from jax.sharding import Mesh, PartitionSpec as P

EXPERTS = 8
CAP = 24
CHUNKS = (384, 256, 256)
VMEM = pl.BlockSpec(memory_space=pltpu.VMEM)


def place_matrices(ids_ref):
    ids = ids_ref[...]
    tokens = ids.shape[1]
    experts = lax.broadcasted_iota(jnp.int32, (EXPERTS, tokens), 0)
    first = (ids[0:1, :] == experts).astype(jnp.float32)
    second = (ids[1:2, :] == experts).astype(jnp.float32)
    before = (
        lax.broadcasted_iota(jnp.int32, (tokens, tokens), 0)
        < lax.broadcasted_iota(jnp.int32, (tokens, tokens), 1)
    ).astype(jnp.float32)
    ahead_first = jnp.dot(first, before, preferred_element_type=jnp.float32)
    ahead_second = jnp.dot(second, before, preferred_element_type=jnp.float32)
    ahead_second = ahead_second + jnp.sum(first, axis=1, keepdims=True)
    place_first = jnp.sum(first * ahead_first, axis=0, keepdims=True).astype(jnp.int32)
    place_second = jnp.sum(second * ahead_second, axis=0, keepdims=True).astype(jnp.int32)
    rows = lax.broadcasted_iota(jnp.int32, (EXPERTS * CAP, tokens), 0)
    return (
        rows == ids[0:1, :] * CAP + place_first,
        rows == ids[1:2, :] * CAP + place_second,
    )


def pack_grad_kernel(ids_ref, prob_ref, grad_ref, out_ref):
    first, second = place_matrices(ids_ref)
    prob = prob_ref[...].astype(jnp.float32)
    pick = jnp.where(first, prob[0:1, :], 0.0) + jnp.where(second, prob[1:2, :], 0.0)
    packed = jnp.dot(
        pick.astype(jnp.bfloat16), grad_ref[...], preferred_element_type=jnp.float32
    )
    out_ref[...] = packed.astype(jnp.bfloat16).reshape(out_ref.shape)


def pack_hidden_kernel(chunks, ids_ref, hidden_ref, *out_refs):
    first, second = place_matrices(ids_ref)
    first = jnp.where(first, 1.0, 0.0).astype(jnp.bfloat16)
    second = jnp.where(second, 1.0, 0.0).astype(jnp.bfloat16)
    unit_cols = sum(chunks)
    start = 0
    for width, out_ref in zip(chunks, out_refs):
        for c in range(2):
            for y in range(4):
                at = (y * 2 + c) * unit_cols + start
                packed = jnp.dot(
                    first, hidden_ref[:, 0, at : at + width], preferred_element_type=jnp.float32
                ) + jnp.dot(
                    second, hidden_ref[:, 1, at : at + width], preferred_element_type=jnp.float32
                )
                out_ref[c * 4 + y] = packed.astype(jnp.bfloat16).reshape(EXPERTS, CAP, width)
        start += width


def per_device(out_grad, saved_hidden, combine, expert_ids):
    tok_count, model_width = out_grad.shape
    ids_t, prob_t = expert_ids.T, combine.T
    send_grad = pl.pallas_call(
        pack_grad_kernel,
        out_shape=jax.ShapeDtypeStruct((EXPERTS, CAP, model_width), jnp.bfloat16),
        in_specs=[VMEM] * 3,
        out_specs=VMEM,
    )(ids_t, prob_t, out_grad)
    send_hidden = pl.pallas_call(
        functools.partial(pack_hidden_kernel, CHUNKS),
        out_shape=[
            jax.ShapeDtypeStruct((8, EXPERTS, CAP, width), jnp.bfloat16) for width in CHUNKS
        ],
        in_specs=[VMEM] * 2,
        out_specs=[VMEM] * len(CHUNKS),
    )(ids_t, saved_hidden)

    exchange = functools.partial(lax.all_to_all, split_axis=0, concat_axis=0, tiled=True)
    by_z = exchange(send_grad, "z")
    by_y = exchange(jnp.broadcast_to(by_z[None], (4, *by_z.shape)), "y")
    by_core = exchange(jnp.broadcast_to(by_y[None], (2, *by_y.shape)), "core")
    grad_rows = by_core.reshape(-1, model_width)
    contract_rows = (((0,), (0,)), ((), ()))
    pieces = []
    for width, piece in zip(CHUNKS, send_hidden):
        arrived = exchange(piece.reshape(64, CAP, width), ("core", "y", "z"))
        hidden_rows = arrived.reshape(-1, width)
        part = lax.dot_general(
            hidden_rows, grad_rows, contract_rows, preferred_element_type=jnp.float32
        ).astype(jnp.bfloat16)
        part = jnp.moveaxis(part.reshape(width, 4, model_width // 4), 1, 0)
        pieces.append(exchange(part, "rep").astype(jnp.float32).sum(axis=0))
    return jnp.concatenate(pieces, axis=0)


def solution(mesh):
    wide = Mesh(mesh.devices.reshape(4, 8, 4, 2), ("rep", "z", "y", "core"))
    rows = ("rep", "z", "y", "core")
    in_specs = (P(rows, None), P(rows, None, None), P(rows, None), P(rows, None))
    out_specs = P(("z", "y", "core"), "rep")
    return jax.shard_map(
        per_device, mesh=wide, in_specs=in_specs, out_specs=out_specs, check_vma=False
    )
```

time: 328 us -> 246 us (0.75)
  waiting for transfers between devices: 186 us -> 74.2 us
  blocking collectives: 47.3 us -> 109 us
  local copies, waits for them, and re-layouts: 53.5 us -> 7.83 us
  Pallas kernels: 0 us -> 9.37 us
  matrix products: 8.38 us -> 15 us
    all_to_all x3 -> x5, waiting for transfers between devices: 186 us -> 74.2 us  [the longest x3 32.9 us: per_device(): pieces.append(exchange(part, 'rep').astype(jnp.float32).sum(axis=0))]
    all_to_all x1 -> x4, blocking collectives: 47.3 us -> 109 us  [the longest x2 59.4 us: per_device(): arrived = exchange(piece.reshape(64, CAP, width), ('core', 'y', 'z'))]
    scatter x5 -> x0, local copies, waits for them, and re-layouts: 39.3 us -> none  [the longest x1 17 us: per_device(): jnp.zeros((EXPERTS, CAP, model_width), jnp.bfloat16)]
    pallas_call x0 -> x2, Pallas kernels: none -> 9.37 us  [the longest x1 7.02 us: per_device(): pl.pallas_call(functools.partial(pack_hidden_kernel, CHUNKS), out_shape=[...]
    dot_general x1 -> x3, matrix products: 8.38 us -> 15 us  [per_device(): lax.dot_general(hidden_rows, grad_rows, contract_rows, preferred_element_...]
    reshape x4 -> x3, local copies, waits for them, and re-layouts: 6.83 us -> 3.47 us  [per_device(): part = jnp.moveaxis(part.reshape(width, 4, model_width // 4), 1, 0)]
    all_to_all x3 -> x5, starting transfers between devices: 28.7 us -> 25.9 us  [the longest x3 11.6 us: per_device(): pieces.append(exchange(part, 'rep').astype(jnp.float32).sum(axis=0))]
  transfers between devices with their start and end apart: 3 -> 5, of which waited for: 2 -> 5; matrix products, arithmetic and copies ran while one was open for 12% -> 8% of each run, Pallas kernels for 0% -> 3%
where the time goes in v1:
time: 246 us; the launch traced here: 243 us
  blocking collectives  109 us (44%)
  waiting for transfers between devices  74.2 us (30%)
  starting transfers between devices  25.9 us (11%)
  matrix products  15 us (6%)
  Pallas kernels  9.37 us (4%)
  local copies, waits for them, and re-layouts  7.83 us (3%)
    all_to_all x2, blocking collectives, per_device(): arrived = exchange(piece.reshape(64, CAP, width), ('core', 'y', 'z'))  59.4 us
    all_to_all x1, blocking collectives, per_device(): by_y = exchange(jnp.broadcast_to(by_z[None], (4, *by_z.shape)), 'y')  39.8 us
    all_to_all x3, waiting for transfers between devices, per_device(): pieces.append(exchange(part, 'rep').astype(jnp.float32).sum(axis=0))  32.9 us
    all_to_all x1, waiting for transfers between devices, per_device(): arrived = exchange(piece.reshape(64, CAP, width), ('core', 'y', 'z'))  26.6 us
    dot_general x3, matrix products, per_device(): lax.dot_general(hidden_rows, grad_rows, contract_rows, preferred_element_...  15 us
    all_to_all x1, waiting for transfers between devices, per_device(): by_z = exchange(send_grad, 'z')  14.6 us
    all_to_all x3, starting transfers between devices, per_device(): pieces.append(exchange(part, 'rep').astype(jnp.float32).sum(axis=0))  11.6 us
    all_to_all x1, blocking collectives, per_device(): by_core = exchange(jnp.broadcast_to(by_y[None], (2, *by_y.shape)), 'core')  9.97 us
  transfers between devices with their start and end apart: 5, of which 5 were waited for; matrix products, arithmetic and copies ran while one was open for 8% of the time, Pallas kernels for 3%

profile of v1, /device:TPU:40, one launch (start us, length us, event | category | flops | bytes accessed | tf_op | source)
XLA Modules:
  0.0 243.4 jit_solution(16622886173677318799)
XLA Ops:
  0.0 2.3 shard_map.47
  2.3 8.6 %all-to-all-start.1 = ((bf16[8,24,2048]{2,1,0:T(8,128)(2,1)}), bf16[8,24,2048]{2,1,0:T(8,128)(2,1)S(1)}, u32[]{:S(2)}, u32[]{:S(2)}) async-start(bf16[8,24,2048]{2,1,0:T(8,128)(2,1)} %shard_map.47), calls=%async_computation.1 | async-start | bytes 1572864 | tf_op jit(solution)/shard_map/all_to_all | solution.py:86
  10.9 7.0 %shard_map.46 = (bf16[8,8,24,384]{3,2,1,0:T(8,128)(2,1)}, bf16[8,8,24,256]{3,2,1,0:T(8,128)(2,1)}, bf16[8,8,24,256]{3,2,1,0:T(8,128)(2,1)}) custom-call(s32[2,64]{1,0:T(2,128)} %bitcast.50, bf16[64,2,7168]{2,1,0:T(2,128)(2,1)} %hidden_ref.1), custom_call_target="tpu_custom_call" | custom-call | tf_op jit(solution)/shard_map/pallas_call | solution.py:76
  17.9 0.0 copy-start.3
  17.9 14.6 %all-to-all-done.1 = bf16[8,24,2048]{2,1,0:T(8,128)(2,1)S(1)} async-done(((bf16[8,24,2048]{2,1,0:T(8,128)(2,1)}), bf16[8,24,2048]{2,1,0:T(8,128)(2,1)S(1)}, u32[]{:S(2)}, u32[]{:S(2)}) %all-to-all-start.1) | async-done | bytes 786464 | tf_op jit(solution)/shard_map/all_to_all | solution.py:86
  32.6 30.3 %all_to_all.45 = bf16[64,24,256]{2,1,0:T(8,128)(2,1)S(1)} all-to-all(bf16[64,24,256]{2,1,0:T(8,128)(2,1)} %bitcast.48), channel_id=1, replica_groups=mesh['rep'=4,'z'=8,'y'=4,'core'=2] {'core','y','z'}, dimensions={0} | all-to-all | bytes 1572864 | tf_op jit(solution)/shard_map/all_to_all | solution.py:93
  62.9 0.0 copy-done.3
  62.9 29.1 %all_to_all.46 = bf16[64,24,256]{2,1,0:T(8,128)(2,1)S(1)} all-to-all(bf16[64,24,256]{2,1,0:T(8,128)(2,1)S(1)} %bitcast.47), channel_id=1, replica_groups=mesh['rep'=4,'z'=8,'y'=4,'core'=2] {'core','y','z'}, dimensions={0} | all-to-all | bytes 1572864 | tf_op jit(solution)/shard_map/all_to_all | solution.py:93
  92.0 0.4 broadcast_in_dim.4
  92.3 39.8 %all_to_all.47 = bf16[4,8,24,2048]{3,2,1,0:T(8,128)(2,1)S(1)} all-to-all(bf16[4,8,24,2048]{3,2,1,0:T(8,128)(2,1)S(1)} %broadcast_in_dim.4), channel_id=1, replica_groups=mesh['rep'=4,'z'=8,'y'=4,'core'=2] {'y'}, dimensions={0} | all-to-all | bytes 6291456 | tf_op jit(solution)/shard_map/all_to_all | solution.py:87
  132.1 0.9 broadcast_in_dim.5
  133.1 10.0 %all_to_all.48 = bf16[2,4,8,24,2048]{4,3,2,1,0:T(8,128)(2,1)} all-to-all(bf16[2,4,8,24,2048]{4,3,2,1,0:T(8,128)(2,1)S(1)} %broadcast_in_dim.5), channel_id=1, replica_groups=mesh['rep'=4,'z'=8,'y'=4,'core'=2] {'core'}, dimensions={0} | all-to-all | bytes 12582912 | tf_op jit(solution)/shard_map/all_to_all | solution.py:88
  143.1 5.8 %all-to-all-start = ((bf16[64,24,384]{2,1,0:T(8,128)(2,1)}), bf16[64,24,384]{2,1,0:T(8,128)(2,1)S(1)}, u32[]{:S(2)}, u32[]{:S(2)}) async-start(bf16[64,24,384]{2,1,0:T(8,128)(2,1)} %bitcast.46), calls=%async_computation | async-start | bytes 2359296 | tf_op jit(solution)/shard_map/all_to_all | solution.py:93
  148.8 4.6 %convolution_convert_fusion.1 = bf16[256,2048]{1,0:T(8,128)(2,1)S(1)} fusion(bf16[1536,256]{1,0:T(8,128)(2,1)S(1)} %bitcast.40, bf16[1536,2048]{1,0:T(8,128)(2,1)} %bitcast.36), kind=kOutput, calls=%fused_computation.2 | convolution fusion | flops 1611137024 | bytes 8126464 | tf_op jit(solution)/shard_map/dot_general | solution.py:95
  153.4 1.1 copy.15
  154.5 26.6 %all-to-all-done = bf16[64,24,384]{2,1,0:T(8,128)(2,1)S(1)} async-done(((bf16[64,24,384]{2,1,0:T(8,128)(2,1)}), bf16[64,24,384]{2,1,0:T(8,128)(2,1)S(1)}, u32[]{:S(2)}, u32[]{:S(2)}) %all-to-all-start) | async-done | bytes 1179680 | tf_op jit(solution)/shard_map/all_to_all | solution.py:93
  181.2 0.0 copy-start.2
  181.2 1.0 copy-done.2
  182.2 4.3 %all-to-all-start.8 = ((bf16[4,256,512]{2,1,0:T(8,128)(2,1)}), bf16[4,256,512]{2,1,0:T(8,128)(2,1)S(1)}, u32[]{:S(2)}, u32[]{:S(2)}) async-start(bf16[4,256,512]{2,1,0:T(8,128)(2,1)} %bitcast.33), calls=%async_computation.8 | async-start | bytes 2097152 | tf_op jit(solution)/shard_map/all_to_all | solution.py:99
  186.5 4.6 %convolution_convert_fusion.2 = bf16[256,2048]{1,0:T(8,128)(2,1)S(1)} fusion(bf16[1536,256]{1,0:T(8,128)(2,1)S(1)} %bitcast.39, bf16[1536,2048]{1,0:T(8,128)(2,1)} %bitcast.37), kind=kOutput, calls=%fused_computation.3 | convolution fusion | flops 1611137024 | bytes 8126464 | tf_op jit(solution)/shard_map/dot_general | solution.py:95
  191.1 1.1 copy.16
  192.2 9.1 %all-to-all-done.8 = bf16[4,256,512]{2,1,0:T(8,128)(2,1)S(1)} async-done(((bf16[4,256,512]{2,1,0:T(8,128)(2,1)}), bf16[4,256,512]{2,1,0:T(8,128)(2,1)S(1)}, u32[]{:S(2)}, u32[]{:S(2)}) %all-to-all-start.8) | async-done | bytes 1048608 | tf_op jit(solution)/shard_map/all_to_all | solution.py:99
  201.3 3.7 %all-to-all-start.6 = ((bf16[4,256,512]{2,1,0:T(8,128)(2,1)}), bf16[4,256,512]{2,1,0:T(8,128)(2,1)S(1)}, u32[]{:S(2)}, u32[]{:S(2)}) async-start(bf16[4,256,512]{2,1,0:T(8,128)(2,1)} %bitcast.41), calls=%async_computation.6 | async-start | bytes 2097152 | tf_op jit(solution)/shard_map/all_to_all | solution.py:99
  205.0 5.8 %convolution_convert_fusion = bf16[384,2048]{1,0:T(8,128)(2,1)S(1)} fusion(bf16[1536,384]{1,0:T(8,128)(2,1)} %bitcast.45, bf16[1536,2048]{1,0:T(8,128)(2,1)} %bitcast.38), kind=kOutput, calls=%fused_computation.1 | convolution fusion | flops 2416705536 | bytes 9043968 | tf_op jit(solution)/shard_map/dot_general | solution.py:95
  210.8 1.3 copy.14
  212.0 6.6 %all-to-all-done.6 = bf16[4,256,512]{2,1,0:T(8,128)(2,1)S(1)} async-done(((bf16[4,256,512]{2,1,0:T(8,128)(2,1)}), bf16[4,256,512]{2,1,0:T(8,128)(2,1)S(1)}, u32[]{:S(2)}, u32[]{:S(2)}) %all-to-all-start.6) | async-done | bytes 1048608 | tf_op jit(solution)/shard_map/all_to_all | solution.py:99
  218.7 0.0 copy-start
  218.7 1.0 copy-done
  219.6 3.6 %all-to-all-start.4 = ((bf16[4,384,512]{2,1,0:T(8,128)(2,1)}), bf16[4,384,512]{2,1,0:T(8,128)(2,1)S(1)}, u32[]{:S(2)}, u32[]{:S(2)}) async-start(bf16[4,384,512]{2,1,0:T(8,128)(2,1)} %bitcast.31), calls=%async_computation.4 | async-start | bytes 3145728 | tf_op jit(solution)/shard_map/all_to_all | solution.py:99
  223.2 0.0 copy-start.1
  223.2 0.1 convert_reduce_fusion.1
  223.4 1.1 copy-done.1
  224.4 0.1 convert_reduce_fusion.2
  224.6 17.3 %all-to-all-done.4 = bf16[4,384,512]{2,1,0:T(8,128)(2,1)S(1)} async-done(((bf16[4,384,512]{2,1,0:T(8,128)(2,1)}), bf16[4,384,512]{2,1,0:T(8,128)(2,1)S(1)}, u32[]{:S(2)}, u32[]{:S(2)}) %all-to-all-start.4) | async-done | bytes 1572896 | tf_op jit(solution)/shard_map/all_to_all | solution.py:99
  241.8 0.2 convert_reduce_fusion
  242.1 1.4 pad_maximum_fusion
Async XLA Ops:
  2.3 30.2 %all-to-all-start.1 = ((bf16[8,24,2048]{2,1,0:T(8,128)(2,1)}), bf16[8,24,2048]{2,1,0:T(8,128)(2,1)S(1)}, u32[]{:S(2)}, u32[]{:S(2)}) async-start(bf16[8,24,2048]{2,1,0:T(8,128)(2,1)} %shard_map.47), calls=%async_computation.1 | async-start | bytes 1572864 | tf_op jit(solution)/shard_map/all_to_all | solution.py:86
  17.9 44.9 %copy-start.3 = (bf16[8,8,24,256]{3,2,1,0:T(8,128)(2,1)S(1)}, bf16[8,8,24,256]{3,2,1,0:T(8,128)(2,1)}, u32[]{:S(2)}) copy-start(bf16[8,8,24,256]{3,2,1,0:T(8,128)(2,1)} %get-tuple-element.9) | copy-start | bytes 2359300
  143.1 38.1 %all-to-all-start = ((bf16[64,24,384]{2,1,0:T(8,128)(2,1)}), bf16[64,24,384]{2,1,0:T(8,128)(2,1)S(1)}, u32[]{:S(2)}, u32[]{:S(2)}) async-start(bf16[64,24,384]{2,1,0:T(8,128)(2,1)} %bitcast.46), calls=%async_computation | async-start | bytes 2359296 | tf_op jit(solution)/shard_map/all_to_all | solution.py:93
  181.2 1.0 copy-start.2
  182.2 19.1 %all-to-all-start.8 = ((bf16[4,256,512]{2,1,0:T(8,128)(2,1)}), bf16[4,256,512]{2,1,0:T(8,128)(2,1)S(1)}, u32[]{:S(2)}, u32[]{:S(2)}) async-start(bf16[4,256,512]{2,1,0:T(8,128)(2,1)} %bitcast.33), calls=%async_computation.8 | async-start | bytes 2097152 | tf_op jit(solution)/shard_map/all_to_all | solution.py:99
  201.3 17.4 %all-to-all-start.6 = ((bf16[4,256,512]{2,1,0:T(8,128)(2,1)}), bf16[4,256,512]{2,1,0:T(8,128)(2,1)S(1)}, u32[]{:S(2)}, u32[]{:S(2)}) async-start(bf16[4,256,512]{2,1,0:T(8,128)(2,1)} %bitcast.41), calls=%async_computation.6 | async-start | bytes 2097152 | tf_op jit(solution)/shard_map/all_to_all | solution.py:99
  218.7 1.0 copy-start
  219.6 22.2 %all-to-all-start.4 = ((bf16[4,384,512]{2,1,0:T(8,128)(2,1)}), bf16[4,384,512]{2,1,0:T(8,128)(2,1)S(1)}, u32[]{:S(2)}, u32[]{:S(2)}) async-start(bf16[4,384,512]{2,1,0:T(8,128)(2,1)} %bitcast.31), calls=%async_computation.4 | async-start | bytes 3145728 | tf_op jit(solution)/shard_map/all_to_all | solution.py:99
  223.2 1.2 copy-start.1
